TPU v7x, 512 devices: a whole 4x8x8 slice. The times are simulated.
512 devices in a mesh: gx: 32 (over x, z), gy: 2 (over y_hi), gz: 8 (over y_lo, core).
Axes of the slice: x: 4, y: 8 (y_hi: 2, y_lo: 4; y = y_hi * 4 + y_lo), z: 8, core: 2. Of those that a mesh axis runs over, the one named last changes fastest.
Arguments:
- coeffs: bfloat16 [16, 1024, 160], P('gz', ('gx', 'gy')), may hold values from -6 to 6
- translations: bfloat16 [16384, 160, 160], P(('gx', 'gz'), 'gy'), may hold values from -0.25 to 0.25
- tmatrix: bfloat16 [1024, 160, 160], P('gx', 'gy'), may hold values from -0.5 to 0.5
- pair_target: int32 [16384], P('gx'), may hold values from 0 to 31
- pair_source: int32 [16384], P('gx'), may hold values from 0 to 1023, as said below
- pair_count: int32 [32], P('gx'), may hold values from 256 to 512, as said below
Outputs:
- result: bfloat16 [16, 1024, 160], P('gz', ('gx', 'gy'))
Inputs may be any that keep to these rules, and one draw needn't show every extreme that they name: `pair_count`: some gx group has all 512 slots live in every draw. The source sphere of a slot of group g lies in group g - 1, g or g + 1 modulo 32, that is pair_source[p] // 32 is one of these.
All inputs are finite; a program needn't handle non-finite values.
Results may differ from a plain program's by a relative error of at most 0.009.
Values may be sent and summed in bfloat16 or wider, within the bound.
No kernel may reach another device: no remote copies, remote signals or barrier semaphores. Data moves between devices by JAX's collectives and lax.ppermute only.
A program may use at most 64 MiB of HBM per device.

v0:
```python
import jax
import jax.numpy as jnp
from jax import lax
from jax.experimental import pallas as pl
from jax.experimental.pallas import tpu as pltpu
from jax.sharding import PartitionSpec as P


LANES = 128
CHUNKS = 2
RUN = 8
COLUMN = ("gy", "gz")
VMEM = pl.BlockSpec(memory_space=pltpu.VMEM)
HBM = pl.BlockSpec(memory_space=pltpu.HBM)
SMEM = pl.BlockSpec(memory_space=pltpu.SMEM)


def pack_rows(full, rest):
    quarter = full.shape[0] // 4
    lane = lax.broadcasted_iota(jnp.int32, (quarter, LANES), 1)
    packed = rest[:quarter]
    for q in range(1, 4):
        part = pltpu.roll(rest[q * quarter : (q + 1) * quarter], 32 * q, 1)
        packed = jnp.where(lane < 32 * q, packed, part)
    return jnp.concatenate([full, packed], axis=0)


def unpack_rest(packed):
    parts = [packed] + [pltpu.roll(packed, LANES - 32 * q, 1) for q in range(1, 4)]
    return jnp.concatenate(parts, axis=0)


def widen(value):
    rows = value.shape[0]
    return jnp.concatenate([value, jnp.zeros((rows, LANES - value.shape[1]), value.dtype)], axis=1)


def pack_kernel(x_ref, out_ref):
    rhs, spheres, length = x_ref.shape
    x = x_ref[...].astype(jnp.float32).reshape(rhs * spheres, length)
    packed = pack_rows(x[:, :LANES], widen(x[:, LANES:])).astype(jnp.bfloat16)
    for d in range(out_ref.shape[0]):
        out_ref[d] = packed


def contract_kernel(
    count_ref, source_hbm, target_hbm, own_ref, odd_ref, even_ref, even_last_ref, mine_ref, other_hbm, near_out,
    source_ref, target_ref, other_ref, full_ref, rest_ref, near_ref, sems,
):
    here = lax.axis_index("gx")
    groups = lax.axis_size("gx")
    core = lax.rem(lax.axis_index("gz"), 2)
    base = pl.multiple_of((lax.axis_index("gz") - core) * mine_ref.shape[0], LANES)
    tables = []
    for i, (hbm, ref) in enumerate(((source_hbm, source_ref), (target_hbm, target_ref))):
        tables.append(pltpu.make_async_copy(hbm.at[pl.ds(base, ref.shape[0])], ref, sems.at[i]))
        tables[i].start()
    part = other_ref.shape[0] // CHUNKS
    copies = []
    for c in range(CHUNKS):
        at = pl.ds(c * part, part)
        copies.append(pltpu.make_async_copy(other_hbm.at[at], other_ref.at[at], sems.at[c + 2]))
        copies[c].start()
    slots = mine_ref.shape[0]
    spheres, rhs, _ = near_out.shape
    length = mine_ref.shape[2]
    members = own_ref.shape[0]
    rows = own_ref.shape[1] * LANES // length
    odd_block = 2 * lax.rem(here, 2)
    for ref, block in ((own_ref, 1), (odd_ref, odd_block), (even_ref, 2 - odd_block)):
        for d in range(members):
            at = pl.ds(pl.multiple_of((block * members + d) * rows, rows), rows)
            piece = ref[d].astype(jnp.float32)
            if ref is even_ref:
                piece = piece + even_last_ref[d].astype(jnp.float32)
            full_ref[at, :] = piece[:rows]
            rest_ref[at, :] = unpack_rest(piece[rows:])
    near_ref[...] = jnp.zeros_like(near_ref)
    for copy in tables:
        copy.wait()
    half = spheres // 2
    assert half & (half - 1) == 0 and groups & (groups - 1) == 0
    shift = half.bit_length() - 1
    offset = (1 - here + groups) * spheres
    live = count_ref[0] - base
    for ref, first in ((mine_ref, core * slots), (other_ref, (1 - core) * slots)):
        for p in range(slots):
            if ref is other_ref and p % part == 0:
                copies[p // part].wait()
            near_by = (source_ref[first + p] + offset) & (groups * spheres - 1)
            start = lax.shift_right_logical(near_by, shift) * (rhs * half) + (near_by & (half - 1))
            at = pl.ds(start, rhs, stride=half)
            x = jnp.concatenate([full_ref[at, :], rest_ref[at, :][:, : length - LANES]], axis=1)
            contrib = lax.dot_general(
                x.astype(jnp.bfloat16), ref[p], (((1,), (1,)), ((), ())),
                preferred_element_type=jnp.float32,
            )
            slot = jnp.where(first + p < live, target_ref[first + p], spheres)
            near_ref[slot] = near_ref[slot] + contrib
    near_out[...] = near_ref[:spheres].astype(jnp.bfloat16)


def apply_kernel(near_ref, tmat_ref, out_ref, full_ref, rest_ref):
    spheres, rhs, _ = near_ref.shape
    half = spheres // 2
    members = out_ref.shape[0]
    rows = full_ref.shape[0] // members
    for s in range(spheres):
        scattered = jnp.dot(near_ref[s], tmat_ref[s], preferred_element_type=jnp.float32)
        at = pl.ds((s // half) * rhs * half + s % half, rhs, stride=half)
        full_ref[at, :] = scattered[:, :LANES]
        rest_ref[at, :] = widen(scattered[:, LANES:])
    for d in range(members):
        at = slice(d * rows, (d + 1) * rows)
        out_ref[d] = pack_rows(full_ref[at, :], rest_ref[at, :]).astype(jnp.bfloat16)


def final_kernel(x_ref, parts_ref, out_ref):
    rhs, spheres, length = x_ref.shape
    rows = rhs * spheres
    total = parts_ref[0].astype(jnp.float32)
    for d in range(1, parts_ref.shape[0]):
        total = total + parts_ref[d].astype(jnp.float32)
    rest = unpack_rest(total[rows:])[:, : length - LANES]
    scattered = jnp.concatenate([total[:rows], rest], axis=1)
    x = x_ref[...].astype(jnp.float32).reshape(rows, length)
    out_ref[...] = (x - scattered).astype(jnp.bfloat16).reshape(rhs, spheres, length)


def limit(mebibytes):
    return pltpu.CompilerParams(vmem_limit_bytes=mebibytes * 2**20)


def cost(flops, size):
    return pl.CostEstimate(flops=flops, bytes_accessed=size, transcendentals=0)


def bf16(*shape):
    return jax.ShapeDtypeStruct(shape, jnp.bfloat16)


def per_device(coeffs, translations, tmatrix, pair_target, pair_source, pair_count):
    groups = lax.axis_size("gx")
    cores = 2
    members = lax.axis_size("gy") * lax.axis_size("gz") // cores
    rhs, spheres, length = coeffs.shape
    rows = rhs * spheres
    packed = rows * length // LANES
    slots, half_length, _ = translations.shape
    group_spheres = tmatrix.shape[0]
    rhs_core = rhs * lax.axis_size("gz") // cores
    even_pairs = [(g, g ^ 1) for g in range(groups)]
    odd_pairs = [(g, (g + 1 if g % 2 else g - 1) % groups) for g in range(groups)]
    sibling = [(i, i ^ 1) for i in range(lax.axis_size("gz"))]
    same_core = [[cores * y + c for y in range(members)] for c in range(cores)]

    def exchange(pieces):
        return lax.all_to_all(
            pieces, COLUMN, split_axis=0, concat_axis=0, tiled=True, axis_index_groups=same_core
        )

    shards = pl.pallas_call(
        pack_kernel, out_shape=bf16(members, packed, LANES), in_specs=[VMEM], out_specs=VMEM,
        compiler_params=limit(2), cost_estimate=cost(10**9, 2**18), name="pack",
    )(coeffs)
    other = lax.ppermute(translations, "gz", sibling)
    own = exchange(shards)
    even_first = lax.ppermute(own, "gx", [p for p in even_pairs if p[0] % RUN < RUN - 2])
    odd = lax.ppermute(own, "gx", odd_pairs)
    even_last = lax.ppermute(own, "gx", [p for p in even_pairs if p[0] % RUN >= RUN - 2])
    window = pltpu.VMEM((3 * members * rows, LANES), jnp.float32)
    near = pl.pallas_call(
        contract_kernel,
        out_shape=bf16(group_spheres, rhs_core, half_length),
        in_specs=[SMEM] + [HBM] * 2 + [VMEM] * 5 + [HBM],
        out_specs=VMEM,
        scratch_shapes=[
            pltpu.SMEM((cores * slots,), jnp.int32),
            pltpu.SMEM((cores * slots,), jnp.int32),
            pltpu.VMEM(translations.shape, jnp.bfloat16),
            window,
            window,
            pltpu.VMEM((group_spheres + 1, rhs_core, half_length), jnp.float32),
            pltpu.SemaphoreType.DMA((CHUNKS + 2,)),
        ],
        compiler_params=limit(10),
        cost_estimate=cost(4 * rhs_core * translations.size, 4 * translations.size),
        name="contract",
    )(pair_count, pair_source, pair_target, own, odd, even_first, even_last, translations, other)
    parts = pl.pallas_call(
        apply_kernel,
        out_shape=bf16(members, packed, LANES),
        in_specs=[VMEM] * 2,
        out_specs=VMEM,
        scratch_shapes=[pltpu.VMEM((members * rows, LANES), jnp.float32)] * 2,
        compiler_params=limit(4),
        cost_estimate=cost(2 * rhs_core * tmatrix.size, 2 * tmatrix.size),
        name="apply",
    )(near, tmatrix)
    arrived = exchange(parts)
    return pl.pallas_call(
        final_kernel, out_shape=bf16(*coeffs.shape), in_specs=[VMEM] * 2, out_specs=VMEM,
        compiler_params=limit(2), name="final",
    )(coeffs, arrived)


def solution(mesh):
    placed = (
        P("gz", ("gx", "gy"), None),
        P(("gx", "gz"), "gy", None),
        P("gx", "gy", None),
        P("gx"),
        P("gx"),
        P("gx"),
    )
    return jax.shard_map(
        per_device,
        mesh=mesh,
        in_specs=placed,
        out_specs=P("gz", ("gx", "gy"), None),
        check_vma=False,
    )
```

profile of v0, /device:TPU:8, one launch (start us, length us, event | category | flops | bytes accessed | tf_op | source)
XLA Modules:
  0.0 50.6 jit_solution(7686980112746776008)
XLA Ops:
  0.0 0.0 copy-start
  0.0 2.2 %collective-permute-start.3 = (bf16[64,80,160]{2,1,0:T(8,128)(2,1)}, bf16[64,80,160]{2,1,0:T(8,128)(2,1)S(1)}, u32[]{:S(2)}, u32[]{:S(2)}) collective-permute-start(bf16[64,80,160]{2,1,0:T(8,128)(2,1)} %mine_ref.1), channel_id=1, source_target_pairs={{0,1},{1,0},{2,3},{3,2},{4,5},{5,4},{6,7},{7,6},{8,9},{9,8},{10,11... | collective-permute-start | bytes 4915208 | tf_op jit(solution)/shard_map/ppermute | solution.py:166
  2.2 0.0 copy-start.2
  2.2 0.7 %copy-done.2 = bf16[2,16,160]{2,1,0:T(8,128)(2,1)S(1)} copy-done((bf16[2,16,160]{2,1,0:T(8,128)(2,1)S(1)}, bf16[2,16,160]{2,1,0:T(8,128)(2,1)}, u32[]{:S(2)}) %copy-start.2) | copy-done | bytes 10264
  2.9 0.1 pack.1
  3.0 15.7 %all_to_all.10.own_ref = bf16[8,40,128]{2,1,0:T(8,128)(2,1)S(1)} all-to-all(bf16[8,40,128]{2,1,0:T(8,128)(2,1)S(1)} %pack.1), channel_id=1, replica_groups={{0,2,4,6,8,10,12,14},{1,3,5,7,9,11,13,15},{16,18,20,22,24,26,28,30},{17..., dimensions={0} | all-to-all | bytes 163840 | tf_op jit(solution)/shard_map/all_to_all | solution.py:158
  18.6 0.7 %collective-permute-start.2 = (bf16[8,40,128]{2,1,0:T(8,128)(2,1)S(1)}, bf16[8,40,128]{2,1,0:T(8,128)(2,1)S(1)}, u32[]{:S(2)}, u32[]{:S(2)}) collective-permute-start(bf16[8,40,128]{2,1,0:T(8,128)(2,1)S(1)} %all_to_all.10.own_ref), channel_id=1, source_target_pairs={{96,112},{112,96},{224,240},{240,224},{352,368},{368,352},{480,496... | collective-permute-start | bytes 245768 | tf_op jit(solution)/shard_map/ppermute | solution.py:170
  19.3 3.2 %collective-permute-start.1 = (bf16[8,40,128]{2,1,0:T(8,128)(2,1)S(1)}, bf16[8,40,128]{2,1,0:T(8,128)(2,1)S(1)}, u32[]{:S(2)}, u32[]{:S(2)}) collective-permute-start(bf16[8,40,128]{2,1,0:T(8,128)(2,1)S(1)} %all_to_all.10.own_ref), channel_id=1, source_target_pairs={{0,16},{16,0},{32,48},{48,32},{64,80},{80,64},{128,144},{144,128},... | collective-permute-start | bytes 245768 | tf_op jit(solution)/shard_map/ppermute | solution.py:168
  22.5 11.3 %collective-permute-start = (bf16[8,40,128]{2,1,0:T(8,128)(2,1)S(1)}, bf16[8,40,128]{2,1,0:T(8,128)(2,1)S(1)}, u32[]{:S(2)}, u32[]{:S(2)}) collective-permute-start(bf16[8,40,128]{2,1,0:T(8,128)(2,1)S(1)} %all_to_all.10.own_ref), channel_id=1, source_target_pairs={{0,496},{16,32},{32,16},{48,64},{64,48},{80,96},{96,80},{112,128},... | collective-permute-start | bytes 245768 | tf_op jit(solution)/shard_map/ppermute | solution.py:169
  34.5 0.0 copy-start.1
  34.5 0.0 copy-start.3
  34.5 0.0 collective-permute-done.2.even_last_ref
  34.5 0.0 collective-permute-done.1.even_ref
  34.5 1.7 %collective-permute-done.odd_ref = bf16[8,40,128]{2,1,0:T(8,128)(2,1)S(1)} collective-permute-done((bf16[8,40,128]{2,1,0:T(8,128)(2,1)S(1)}, bf16[8,40,128]{2,1,0:T(8,128)(2,1)S(1)}, u32[]{:S(2)}, u32[]{:S(2)}) %collective-permute-start) | collective-permute-done | bytes 81952 | tf_op jit(solution)/shard_map/ppermute | solution.py:169
  36.2 0.0 collective-permute-done.3.other_hbm
  36.2 0.0 copy-done
  36.2 0.0 copy-done.4
  36.2 0.0 copy-done.5
  36.2 2.4 %contract.1.near_ref = bf16[32,8,80]{2,1,0:T(8,128)(2,1)S(1)} custom-call(s32[1]{0:T(128)S(6)} %copy.7.count_ref, s32[512]{0:T(512)S(1)} %copy-done.4, s32[512]{0:T(512)S(1)} %copy-done.5, bf16[8,40,128]{2,1,0:T(8,128)(2,1)S(1)} %all_to_all.10.own_ref, bf16[8,40,128]{2,1,0:T(8,128)(2,1)S(1)} %collective-permute-done.odd_ref, ...), custom_call_target="tpu_custom_call" | custom-call | flops 26214400 | bytes 3276800 | tf_op jit(solution)/shard_map/contract/pallas_call | solution.py:172
  38.7 0.0 copy-done.1
  38.7 0.4 apply.1
  39.0 10.9 %all_to_all.11.parts_ref = bf16[8,40,128]{2,1,0:T(8,128)(2,1)S(1)} all-to-all(bf16[8,40,128]{2,1,0:T(8,128)(2,1)S(1)} %apply.1), channel_id=1, replica_groups={{0,2,4,6,8,10,12,14},{1,3,5,7,9,11,13,15},{16,18,20,22,24,26,28,30},{17..., dimensions={0} | all-to-all | bytes 163840 | tf_op jit(solution)/shard_map/all_to_all | solution.py:158
  50.0 0.0 copy-done.3
  50.0 0.7 %final.1 = bf16[2,16,160]{2,1,0:T(8,128)(2,1)} custom-call(bf16[2,16,160]{2,1,0:T(8,128)(2,1)S(1)} %copy-done.3, bf16[8,40,128]{2,1,0:T(8,128)(2,1)S(1)} %all_to_all.11.parts_ref), custom_call_target="tpu_custom_call" | custom-call | tf_op jit(solution)/shard_map/final/pallas_call | solution.py:201
  (2 shorter events, 0.0 us)
Async XLA Ops:
  0.0 36.2 %copy-start = (bf16[64,80,160]{2,1,0:T(8,128)(2,1)S(1)}, bf16[64,80,160]{2,1,0:T(8,128)(2,1)}, u32[]{:S(2)}) copy-start(bf16[64,80,160]{2,1,0:T(8,128)(2,1)} %mine_ref.1) | copy-start | bytes 4915204
  0.0 36.2 %collective-permute-start.3 = (bf16[64,80,160]{2,1,0:T(8,128)(2,1)}, bf16[64,80,160]{2,1,0:T(8,128)(2,1)S(1)}, u32[]{:S(2)}, u32[]{:S(2)}) collective-permute-start(bf16[64,80,160]{2,1,0:T(8,128)(2,1)} %mine_ref.1), channel_id=1, source_target_pairs={{0,1},{1,0},{2,3},{3,2},{4,5},{5,4},{6,7},{7,6},{8,9},{9,8},{10,11... | collective-permute-start | bytes 4915208 | tf_op jit(solution)/shard_map/ppermute | solution.py:166
  2.2 0.7 %copy-start.2 = (bf16[2,16,160]{2,1,0:T(8,128)(2,1)S(1)}, bf16[2,16,160]{2,1,0:T(8,128)(2,1)}, u32[]{:S(2)}) copy-start(bf16[2,16,160]{2,1,0:T(8,128)(2,1)} %x_ref.3) | copy-start | bytes 30724
  2.9 33.3 %copy-start.4 = (s32[512]{0:T(512)S(1)}, s32[512]{0:T(512)}, u32[]{:S(2)}) copy-start(s32[512]{0:T(512)} %source_hbm.1) | copy-start | bytes 6148
  2.9 33.3 %copy-start.5 = (s32[512]{0:T(512)S(1)}, s32[512]{0:T(512)}, u32[]{:S(2)}) copy-start(s32[512]{0:T(512)} %target_hbm.1) | copy-start | bytes 6148
  18.6 15.8 %collective-permute-start.2 = (bf16[8,40,128]{2,1,0:T(8,128)(2,1)S(1)}, bf16[8,40,128]{2,1,0:T(8,128)(2,1)S(1)}, u32[]{:S(2)}, u32[]{:S(2)}) collective-permute-start(bf16[8,40,128]{2,1,0:T(8,128)(2,1)S(1)} %all_to_all.10.own_ref), channel_id=1, source_target_pairs={{96,112},{112,96},{224,240},{240,224},{352,368},{368,352},{480,496... | collective-permute-start | bytes 245768 | tf_op jit(solution)/shard_map/ppermute | solution.py:170
  19.3 15.2 %collective-permute-start.1 = (bf16[8,40,128]{2,1,0:T(8,128)(2,1)S(1)}, bf16[8,40,128]{2,1,0:T(8,128)(2,1)S(1)}, u32[]{:S(2)}, u32[]{:S(2)}) collective-permute-start(bf16[8,40,128]{2,1,0:T(8,128)(2,1)S(1)} %all_to_all.10.own_ref), channel_id=1, source_target_pairs={{0,16},{16,0},{32,48},{48,32},{64,80},{80,64},{128,144},{144,128},... | collective-permute-start | bytes 245768 | tf_op jit(solution)/shard_map/ppermute | solution.py:168
  22.5 13.7 %collective-permute-start = (bf16[8,40,128]{2,1,0:T(8,128)(2,1)S(1)}, bf16[8,40,128]{2,1,0:T(8,128)(2,1)S(1)}, u32[]{:S(2)}, u32[]{:S(2)}) collective-permute-start(bf16[8,40,128]{2,1,0:T(8,128)(2,1)S(1)} %all_to_all.10.own_ref), channel_id=1, source_target_pairs={{0,496},{16,32},{32,16},{48,64},{64,48},{80,96},{96,80},{112,128},... | collective-permute-start | bytes 245768 | tf_op jit(solution)/shard_map/ppermute | solution.py:169
  34.5 4.2 %copy-start.1 = (bf16[32,80,160]{2,1,0:T(8,128)(2,1)S(1)}, bf16[32,80,160]{2,1,0:T(8,128)(2,1)}, u32[]{:S(2)}) copy-start(bf16[32,80,160]{2,1,0:T(8,128)(2,1)} %tmat_ref.1) | copy-start | bytes 2457604
  34.5 15.5 %copy-start.3 = (bf16[2,16,160]{2,1,0:T(8,128)(2,1)S(1)}, bf16[2,16,160]{2,1,0:T(8,128)(2,1)}, u32[]{:S(2)}) copy-start(bf16[2,16,160]{2,1,0:T(8,128)(2,1)} %x_ref.3) | copy-start | bytes 30724
where the time goes:
time: 51 us; the launch traced here: 50.6 us
  blocking collectives  26.6 us (52%)
  starting transfers between devices  17.3 us (34%)
  Pallas kernels  3.54 us (7%)
  waiting for transfers between devices  1.72 us (3%)
  between operations  0.75 us (1%)
  local copies, waits for them, and re-layouts  0.74 us (1%)
    all_to_all x2, blocking collectives, exchange(): lax.all_to_all(pieces, COLUMN, split_axis=0, concat_axis=0, tiled=True, a...  26.6 us
    ppermute x1, starting transfers between devices, per_device(): odd = lax.ppermute(own, 'gx', odd_pairs)  11.3 us
    ppermute x1, starting transfers between devices, per_device(): lax.ppermute(own, 'gx', [p for p in even_pairs if p[0] % RUN < RUN - 2])  3.18 us
    pallas_call x1, Pallas kernels, per_device(): pl.pallas_call(contract_kernel, out_shape=bf16(group_spheres, rhs_core, h...  2.41 us
    ppermute x1, starting transfers between devices, per_device(): other = lax.ppermute(translations, 'gz', sibling)  2.17 us
    ppermute x1, waiting for transfers between devices, per_device(): odd = lax.ppermute(own, 'gx', odd_pairs)  1.71 us
  transfers between devices with their start and end apart: 4, of which 1 were waited for; matrix products, arithmetic and copies ran while one was open for 0% of the time, Pallas kernels for 0%

commit v1 on v0

--- a/solution.py
+++ b/solution.py
@@ -104,7 +104,7 @@
     spheres, rhs, _ = near_ref.shape
     half = spheres // 2
     members = out_ref.shape[0]
-    rows = full_ref.shape[0] // members
+    rows = out_ref.shape[1] * LANES // tmat_ref.shape[2]
     for s in range(spheres):
         scattered = jnp.dot(near_ref[s], tmat_ref[s], preferred_element_type=jnp.float32)
         at = pl.ds((s // half) * rhs * half + s % half, rhs, stride=half)
@@ -168,7 +168,7 @@
     even_first = lax.ppermute(own, "gx", [p for p in even_pairs if p[0] % RUN < RUN - 2])
     odd = lax.ppermute(own, "gx", odd_pairs)
     even_last = lax.ppermute(own, "gx", [p for p in even_pairs if p[0] % RUN >= RUN - 2])
-    window = pltpu.VMEM((3 * members * rows, LANES), jnp.float32)
+    window = pltpu.VMEM((3 * members * rows + spheres, LANES), jnp.float32)
     near = pl.pallas_call(
         contract_kernel,
         out_shape=bf16(group_spheres, rhs_core, half_length),
@@ -192,7 +192,7 @@
         out_shape=bf16(members, packed, LANES),
         in_specs=[VMEM] * 2,
         out_specs=VMEM,
-        scratch_shapes=[pltpu.VMEM((members * rows, LANES), jnp.float32)] * 2,
+        scratch_shapes=[pltpu.VMEM((members * rows + spheres, LANES), jnp.float32)] * 2,
         compiler_params=limit(4),
         cost_estimate=cost(2 * rhs_core * tmatrix.size, 2 * tmatrix.size),
         name="apply",

time: 51 us -> 51 us (level)
  no operation moved by 1% of the time
where the time goes in v1:
time: 51 us; the launch traced here: 50.6 us
  blocking collectives  26.6 us (52%)
  starting transfers between devices  17.3 us (34%)
  Pallas kernels  3.54 us (7%)
  waiting for transfers between devices  1.72 us (3%)
  between operations  0.75 us (1%)
  local copies, waits for them, and re-layouts  0.74 us (1%)
    all_to_all x2, blocking collectives, exchange(): lax.all_to_all(pieces, COLUMN, split_axis=0, concat_axis=0, tiled=True, a...  26.6 us
    ppermute x1, starting transfers between devices, per_device(): odd = lax.ppermute(own, 'gx', odd_pairs)  11.3 us
    ppermute x1, starting transfers between devices, per_device(): lax.ppermute(own, 'gx', [p for p in even_pairs if p[0] % RUN < RUN - 2])  3.18 us
    pallas_call x1, Pallas kernels, per_device(): pl.pallas_call(contract_kernel, out_shape=bf16(group_spheres, rhs_core, h...  2.41 us
    ppermute x1, starting transfers between devices, per_device(): other = lax.ppermute(translations, 'gz', sibling)  2.17 us
    ppermute x1, waiting for transfers between devices, per_device(): odd = lax.ppermute(own, 'gx', odd_pairs)  1.71 us
  transfers between devices with their start and end apart: 4, of which 1 were waited for; matrix products, arithmetic and copies ran while one was open for 0% of the time, Pallas kernels for 0%

profile of v1, /device:TPU:8, one launch (start us, length us, event | category | flops | bytes accessed | tf_op | source)
XLA Modules:
  0.0 50.6 jit_solution(11135032886965854843)
XLA Ops:
  0.0 0.0 copy-start
  0.0 2.2 %collective-permute-start.3 = (bf16[64,80,160]{2,1,0:T(8,128)(2,1)}, bf16[64,80,160]{2,1,0:T(8,128)(2,1)S(1)}, u32[]{:S(2)}, u32[]{:S(2)}) collective-permute-start(bf16[64,80,160]{2,1,0:T(8,128)(2,1)} %mine_ref.1), channel_id=1, source_target_pairs={{0,1},{1,0},{2,3},{3,2},{4,5},{5,4},{6,7},{7,6},{8,9},{9,8},{10,11... | collective-permute-start | bytes 4915208 | tf_op jit(solution)/shard_map/ppermute | solution.py:166
  2.2 0.0 copy-start.2
  2.2 0.7 %copy-done.2 = bf16[2,16,160]{2,1,0:T(8,128)(2,1)S(1)} copy-done((bf16[2,16,160]{2,1,0:T(8,128)(2,1)S(1)}, bf16[2,16,160]{2,1,0:T(8,128)(2,1)}, u32[]{:S(2)}) %copy-start.2) | copy-done | bytes 10264
  2.9 0.1 pack.1
  3.0 15.7 %all_to_all.10.own_ref = bf16[8,40,128]{2,1,0:T(8,128)(2,1)S(1)} all-to-all(bf16[8,40,128]{2,1,0:T(8,128)(2,1)S(1)} %pack.1), channel_id=1, replica_groups={{0,2,4,6,8,10,12,14},{1,3,5,7,9,11,13,15},{16,18,20,22,24,26,28,30},{17..., dimensions={0} | all-to-all | bytes 163840 | tf_op jit(solution)/shard_map/all_to_all | solution.py:158
  18.6 0.7 %collective-permute-start.2 = (bf16[8,40,128]{2,1,0:T(8,128)(2,1)S(1)}, bf16[8,40,128]{2,1,0:T(8,128)(2,1)S(1)}, u32[]{:S(2)}, u32[]{:S(2)}) collective-permute-start(bf16[8,40,128]{2,1,0:T(8,128)(2,1)S(1)} %all_to_all.10.own_ref), channel_id=1, source_target_pairs={{96,112},{112,96},{224,240},{240,224},{352,368},{368,352},{480,496... | collective-permute-start | bytes 245768 | tf_op jit(solution)/shard_map/ppermute | solution.py:170
  19.3 3.2 %collective-permute-start.1 = (bf16[8,40,128]{2,1,0:T(8,128)(2,1)S(1)}, bf16[8,40,128]{2,1,0:T(8,128)(2,1)S(1)}, u32[]{:S(2)}, u32[]{:S(2)}) collective-permute-start(bf16[8,40,128]{2,1,0:T(8,128)(2,1)S(1)} %all_to_all.10.own_ref), channel_id=1, source_target_pairs={{0,16},{16,0},{32,48},{48,32},{64,80},{80,64},{128,144},{144,128},... | collective-permute-start | bytes 245768 | tf_op jit(solution)/shard_map/ppermute | solution.py:168
  22.5 11.3 %collective-permute-start = (bf16[8,40,128]{2,1,0:T(8,128)(2,1)S(1)}, bf16[8,40,128]{2,1,0:T(8,128)(2,1)S(1)}, u32[]{:S(2)}, u32[]{:S(2)}) collective-permute-start(bf16[8,40,128]{2,1,0:T(8,128)(2,1)S(1)} %all_to_all.10.own_ref), channel_id=1, source_target_pairs={{0,496},{16,32},{32,16},{48,64},{64,48},{80,96},{96,80},{112,128},... | collective-permute-start | bytes 245768 | tf_op jit(solution)/shard_map/ppermute | solution.py:169
  34.5 0.0 copy-start.1
  34.5 0.0 copy-start.3
  34.5 0.0 collective-permute-done.2.even_last_ref
  34.5 0.0 collective-permute-done.1.even_ref
  34.5 1.7 %collective-permute-done.odd_ref = bf16[8,40,128]{2,1,0:T(8,128)(2,1)S(1)} collective-permute-done((bf16[8,40,128]{2,1,0:T(8,128)(2,1)S(1)}, bf16[8,40,128]{2,1,0:T(8,128)(2,1)S(1)}, u32[]{:S(2)}, u32[]{:S(2)}) %collective-permute-start) | collective-permute-done | bytes 81952 | tf_op jit(solution)/shard_map/ppermute | solution.py:169
  36.2 0.0 collective-permute-done.3.other_hbm
  36.2 0.0 copy-done
  36.2 0.0 copy-done.4
  36.2 0.0 copy-done.5
  36.2 2.4 %contract.1.near_ref = bf16[32,8,80]{2,1,0:T(8,128)(2,1)S(1)} custom-call(s32[1]{0:T(128)S(6)} %copy.7.count_ref, s32[512]{0:T(512)S(1)} %copy-done.4, s32[512]{0:T(512)S(1)} %copy-done.5, bf16[8,40,128]{2,1,0:T(8,128)(2,1)S(1)} %all_to_all.10.own_ref, bf16[8,40,128]{2,1,0:T(8,128)(2,1)S(1)} %collective-permute-done.odd_ref, ...), custom_call_target="tpu_custom_call" | custom-call | flops 26214400 | bytes 3276800 | tf_op jit(solution)/shard_map/contract/pallas_call | solution.py:172
  38.7 0.0 copy-done.1
  38.7 0.4 apply.1
  39.0 10.9 %all_to_all.11.parts_ref = bf16[8,40,128]{2,1,0:T(8,128)(2,1)S(1)} all-to-all(bf16[8,40,128]{2,1,0:T(8,128)(2,1)S(1)} %apply.1), channel_id=1, replica_groups={{0,2,4,6,8,10,12,14},{1,3,5,7,9,11,13,15},{16,18,20,22,24,26,28,30},{17..., dimensions={0} | all-to-all | bytes 163840 | tf_op jit(solution)/shard_map/all_to_all | solution.py:158
  50.0 0.0 copy-done.3
  50.0 0.7 %final.1 = bf16[2,16,160]{2,1,0:T(8,128)(2,1)} custom-call(bf16[2,16,160]{2,1,0:T(8,128)(2,1)S(1)} %copy-done.3, bf16[8,40,128]{2,1,0:T(8,128)(2,1)S(1)} %all_to_all.11.parts_ref), custom_call_target="tpu_custom_call" | custom-call | tf_op jit(solution)/shard_map/final/pallas_call | solution.py:201
  (2 shorter events, 0.0 us)
Async XLA Ops:
  0.0 36.2 %copy-start = (bf16[64,80,160]{2,1,0:T(8,128)(2,1)S(1)}, bf16[64,80,160]{2,1,0:T(8,128)(2,1)}, u32[]{:S(2)}) copy-start(bf16[64,80,160]{2,1,0:T(8,128)(2,1)} %mine_ref.1) | copy-start | bytes 4915204
  0.0 36.2 %collective-permute-start.3 = (bf16[64,80,160]{2,1,0:T(8,128)(2,1)}, bf16[64,80,160]{2,1,0:T(8,128)(2,1)S(1)}, u32[]{:S(2)}, u32[]{:S(2)}) collective-permute-start(bf16[64,80,160]{2,1,0:T(8,128)(2,1)} %mine_ref.1), channel_id=1, source_target_pairs={{0,1},{1,0},{2,3},{3,2},{4,5},{5,4},{6,7},{7,6},{8,9},{9,8},{10,11... | collective-permute-start | bytes 4915208 | tf_op jit(solution)/shard_map/ppermute | solution.py:166
  2.2 0.7 %copy-start.2 = (bf16[2,16,160]{2,1,0:T(8,128)(2,1)S(1)}, bf16[2,16,160]{2,1,0:T(8,128)(2,1)}, u32[]{:S(2)}) copy-start(bf16[2,16,160]{2,1,0:T(8,128)(2,1)} %x_ref.3) | copy-start | bytes 30724
  2.9 33.3 %copy-start.4 = (s32[512]{0:T(512)S(1)}, s32[512]{0:T(512)}, u32[]{:S(2)}) copy-start(s32[512]{0:T(512)} %source_hbm.1) | copy-start | bytes 6148
  2.9 33.3 %copy-start.5 = (s32[512]{0:T(512)S(1)}, s32[512]{0:T(512)}, u32[]{:S(2)}) copy-start(s32[512]{0:T(512)} %target_hbm.1) | copy-start | bytes 6148
  18.6 15.8 %collective-permute-start.2 = (bf16[8,40,128]{2,1,0:T(8,128)(2,1)S(1)}, bf16[8,40,128]{2,1,0:T(8,128)(2,1)S(1)}, u32[]{:S(2)}, u32[]{:S(2)}) collective-permute-start(bf16[8,40,128]{2,1,0:T(8,128)(2,1)S(1)} %all_to_all.10.own_ref), channel_id=1, source_target_pairs={{96,112},{112,96},{224,240},{240,224},{352,368},{368,352},{480,496... | collective-permute-start | bytes 245768 | tf_op jit(solution)/shard_map/ppermute | solution.py:170
  19.3 15.2 %collective-permute-start.1 = (bf16[8,40,128]{2,1,0:T(8,128)(2,1)S(1)}, bf16[8,40,128]{2,1,0:T(8,128)(2,1)S(1)}, u32[]{:S(2)}, u32[]{:S(2)}) collective-permute-start(bf16[8,40,128]{2,1,0:T(8,128)(2,1)S(1)} %all_to_all.10.own_ref), channel_id=1, source_target_pairs={{0,16},{16,0},{32,48},{48,32},{64,80},{80,64},{128,144},{144,128},... | collective-permute-start | bytes 245768 | tf_op jit(solution)/shard_map/ppermute | solution.py:168
  22.5 13.7 %collective-permute-start = (bf16[8,40,128]{2,1,0:T(8,128)(2,1)S(1)}, bf16[8,40,128]{2,1,0:T(8,128)(2,1)S(1)}, u32[]{:S(2)}, u32[]{:S(2)}) collective-permute-start(bf16[8,40,128]{2,1,0:T(8,128)(2,1)S(1)} %all_to_all.10.own_ref), channel_id=1, source_target_pairs={{0,496},{16,32},{32,16},{48,64},{64,48},{80,96},{96,80},{112,128},... | collective-permute-start | bytes 245768 | tf_op jit(solution)/shard_map/ppermute | solution.py:169
  34.5 4.2 %copy-start.1 = (bf16[32,80,160]{2,1,0:T(8,128)(2,1)S(1)}, bf16[32,80,160]{2,1,0:T(8,128)(2,1)}, u32[]{:S(2)}) copy-start(bf16[32,80,160]{2,1,0:T(8,128)(2,1)} %tmat_ref.1) | copy-start | bytes 2457604
  34.5 15.5 %copy-start.3 = (bf16[2,16,160]{2,1,0:T(8,128)(2,1)S(1)}, bf16[2,16,160]{2,1,0:T(8,128)(2,1)}, u32[]{:S(2)}) copy-start(bf16[2,16,160]{2,1,0:T(8,128)(2,1)} %x_ref.3) | copy-start | bytes 30724
